TPU v7x, 512 devices: a whole 4x4x16 slice. The times are simulated.
512 devices in a mesh: node: 32 (over y, x, core), row: 16 (over z).
Axes of the slice: x: 4, y: 4, z: 16, core: 2. Of those that a mesh axis runs over, the one named last changes fastest.
Arguments:
- samples: bfloat16 [32, 16384, 384], P('node', 'row'), parts along dimension 0, may hold values from -6 to 6
- column_order: int32 [32, 384], P('node'), parts along dimension 0, may hold values from 0 to 383, each once within a row
- skeleton: int32 [32, 256], P('node'), parts along dimension 0, may hold values from 0 to 16383, as said below
Outputs:
- q_factor: float32 [32, 16384, 384], P('node', 'row'), parts along dimension 0
- interp: bfloat16 [32, 16384, 256], P('node', 'row'), parts along dimension 0
There are 32 independent parts, one for each index of `node`. A program takes and returns all parts, laid end to end along the dimension named above; each array names one. Nothing has to cross between parts.
Inputs may be any that keep to these rules, and one draw needn't show every extreme that they name: `skeleton`: each row names 256 distinct sample rows in ascending order. `column_order`: each row is a permutation.
All inputs are finite; a program needn't handle non-finite values.
Results may differ from a plain program's by a relative error of at most 0.001.
Values sent between devices are 32-bit elements; how exact they have to be, the bound alone decides.
A program may use at most 64 MiB of HBM per device.

v0:
```python
import jax
import jax.numpy as jnp
from jax import lax
from jax.sharding import PartitionSpec as P


def lower_solve(lower, right):
    return jax.scipy.linalg.solve_triangular(lower, right, lower=True)


def upper_solve(lower, right):
    return jax.scipy.linalg.solve_triangular(lower, right, lower=True, trans="T")


def on_device(samples, column_order, skeleton):
    rows_here = samples.shape[1]
    total_rows = rows_here * lax.axis_size("row")
    permuted = jax.vmap(lambda block, order: block[:, order])(samples, column_order)
    gram_local = jnp.einsum("frc,frd->fcd", permuted, permuted, preferred_element_type=jnp.float32)
    offset = lax.axis_index("row") * rows_here
    positions = offset + lax.iota(jnp.int32, rows_here)
    selector = skeleton[:, :, None] == positions[None, None, :]
    picked = jnp.einsum(
        "fkr,frc->fkc", selector.astype(jnp.bfloat16), permuted, preferred_element_type=jnp.float32
    )
    gram, yskel = lax.psum((gram_local, picked), "row")
    lower = jnp.linalg.cholesky(gram / total_rows)
    wide = permuted.astype(jnp.float32)
    q_factor = jnp.swapaxes(jax.vmap(lower_solve)(lower, jnp.swapaxes(wide, 1, 2)), 1, 2)
    qskel = jnp.swapaxes(jax.vmap(lower_solve)(lower, jnp.swapaxes(yskel, 1, 2)), 1, 2)
    small = jnp.einsum("fkc,fjc->fkj", qskel, qskel, precision=lax.Precision.HIGHEST)
    lower_small = jnp.linalg.cholesky(small)
    cross = jnp.einsum("frc,fkc->frk", q_factor, qskel, precision=lax.Precision.HIGHEST)
    inner = jax.vmap(lower_solve)(lower_small, jnp.swapaxes(cross, 1, 2))
    interp = jnp.swapaxes(jax.vmap(upper_solve)(lower_small, inner), 1, 2)
    return (q_factor, interp.astype(jnp.bfloat16))


def solution(mesh):
    placed = (P("node", "row", None), P("node", None), P("node", None))
    return jax.shard_map(
        on_device,
        mesh=mesh,
        in_specs=placed,
        out_specs=(P("node", "row", None), P("node", "row", None)),
        check_vma=False,
    )
```

profile of v0, /device:TPU:6, one launch (start us, length us, event | category | flops | bytes accessed | tf_op | source)
XLA Modules:
  0.0 361.4 jit_solution(16786022696405899431)
XLA Ops:
  9.4 4.7 %gather_fusion = bf16[384,1024]{1,0:T(8,128)(2,1)S(1)} fusion(bf16[1,1024,384]{1,2,0:T(8,128)(2,1)S(1)} %copy.17, s32[384]{0:T(512)S(1)} %fusion.47), kind=kCustom, calls=%fused_computation | custom fusion | bytes 1575936 | tf_op jit(solution)/shard_map/vmap()/gather | solution.py:18
  17.0 144.3 %all-reduce.5.cloned.1.call-done = (f32[1,384,384]{1,2,0:T(8,128)}, f32[1,384,256]{1,2,0:T(8,128)}) async-done(((f32[1,384,384]{1,2,0:T(8,128)}, f32[1,384,256]{1,2,0:T(8,128)}), (f32[1,384,384]{1,2,0:T(8,128)}, f32[1,384,256]{1,2,0:T(8,128)})) %all-reduce.5.cloned.1.call-update) | async-done | bytes 983056 | tf_op jit(solution)/shard_map/psum | solution.py:26
  161.3 2.0 broadcast_multiply_fusion
  165.5 11.7 %custom-call.42 = f32[1,128,128]{2,1,0:T(8,128)S(1)} custom-call(f32[1,128,128]{2,1,0:T(8,128)S(1)} %cholesky.264), custom_call_target="Cholesky" | custom-call | tf_op jit(solution)/shard_map/jit(cholesky)/cholesky | solution.py:27
  177.2 9.8 %custom-call.43 = f32[1,1,128,128]{2,3,1,0:T(8,128)S(1)} custom-call(f32[1,1,128,128]{3,2,1,0:T(8,128)S(1)} %get-tuple-element.55), custom_call_target="InvertDiagBlocksLowerTriangular" | custom-call | tf_op jit(solution)/shard_map/jit(cholesky)/cholesky | solution.py:27
  189.4 11.7 %custom-call.44 = f32[1,128,128]{2,1,0:T(8,128)S(1)} custom-call(f32[1,128,128]{2,1,0:T(8,128)S(1)} %cholesky.268), custom_call_target="Cholesky" | custom-call | tf_op jit(solution)/shard_map/jit(cholesky)/cholesky | solution.py:27
  201.2 10.0 %custom-call.53 = f32[1,1,128,128]{2,3,1,0:T(8,128)S(1)} custom-call(f32[1,1,128,128]{3,2,1,0:T(8,128)S(1)} %get-tuple-element.52), custom_call_target="InvertDiagBlocksLowerTriangular" | custom-call | tf_op jit(solution)/shard_map/jit(cholesky)/cholesky/custom-call.10 | solution.py:27
  212.5 11.7 %custom-call.45 = f32[1,128,128]{2,1,0:T(8,128)S(1)} custom-call(f32[1,128,128]{2,1,0:T(8,128)S(1)} %fusion.19), custom_call_target="Cholesky" | custom-call | tf_op jit(solution)/shard_map/jit(cholesky)/cholesky | solution.py:27
  227.7 7.8 %while.2 = (s32[]{:T(128)}, f32[1,384,384]{2,1,0:T(8,128)S(1)}, s32[3,2]{0,1:T(2,128)S(1)}, f32[3,1,128,128]{3,2,1,0:T(8,128)}, s32[]{:T(128)}) while((s32[]{:T(128)}, f32[1,384,384]{2,1,0:T(8,128)S(1)}, s32[3,2]{0,1:T(2,128)S(1)}, f32[3,1,128,128]{3,2,1,0:T(8,128)}, s32[]{:T(128)}) %tuple.49), condition=%wide.while_cond, body=%wide.while_body.sunk | while | flops 2 | bytes 132205 | solution.py:8
  228.3 2.0 bitcast_dynamic-update-slice_fusion.5
  230.9 2.0 bitcast_dynamic-update-slice_fusion.5
  233.5 2.0 bitcast_dynamic-update-slice_fusion.5
  235.5 30.7 %custom-call.46 = f32[1,3,128,128]{2,3,1,0:T(8,128)S(1)} custom-call(f32[1,3,128,128]{3,2,1,0:T(8,128)} %bitcast.260), custom_call_target="InvertDiagBlocksLowerTriangular" | custom-call | tf_op jit(solution)/shard_map/vmap(jit(_solve_triangular))/triangular_solve | solution.py:8
  269.1 1.5 fusion.16
  275.0 11.7 %custom-call.47 = f32[1,128,128]{2,1,0:T(8,128)S(1)} custom-call(f32[1,128,128]{2,1,0:T(8,128)S(1)} %cholesky.272), custom_call_target="Cholesky" | custom-call | tf_op jit(solution)/shard_map/jit(cholesky)/cholesky | solution.py:32
  289.2 1.5 convolution_bitcast_fusion.4
  292.9 2.7 fusion.2
  296.5 10.8 %custom-call.54 = f32[1,1,128,128]{2,3,1,0:T(8,128)S(1)} custom-call(f32[1,1,128,128]{3,2,1,0:T(8,128)} %get-tuple-element.48), custom_call_target="InvertDiagBlocksLowerTriangular" | custom-call | tf_op jit(solution)/shard_map/jit(cholesky)/cholesky/custom-call.10 | solution.py:32
  307.8 11.7 %custom-call.48 = f32[1,128,128]{2,1,0:T(8,128)S(1)} custom-call(f32[1,128,128]{2,1,0:T(8,128)S(1)} %fusion.18), custom_call_target="Cholesky" | custom-call | tf_op jit(solution)/shard_map/jit(cholesky)/cholesky | solution.py:32
  321.6 5.2 %while.3 = (s32[]{:T(128)}, f32[1,256,256]{2,1,0:T(8,128)S(1)}, s32[2,2]{1,0:T(2,128)S(1)}, f32[2,1,128,128]{3,2,1,0:T(8,128)}, s32[]{:T(128)}) while((s32[]{:T(128)}, f32[1,256,256]{2,1,0:T(8,128)S(1)}, s32[2,2]{1,0:T(2,128)S(1)}, f32[2,1,128,128]{3,2,1,0:T(8,128)}, s32[]{:T(128)}) %tuple.52), condition=%wide.while_cond.1, body=%wide.while_body.1.sunk | while | flops 2 | bytes 132205 | solution.py:12
  322.2 2.0 bitcast_dynamic-update-slice_fusion.6
  324.8 2.0 bitcast_dynamic-update-slice_fusion.6
  326.8 20.7 %custom-call.49 = f32[1,2,128,128]{2,3,1,0:T(8,128)S(1)} custom-call(f32[1,2,128,128]{3,2,1,0:T(8,128)} %bitcast.261), custom_call_target="InvertDiagBlocksLowerTriangular" | custom-call | tf_op jit(solution)/shard_map/vmap(jit(_solve_triangular))/triangular_solve | solution.py:12
  351.1 1.6 copy.27
  (87 shorter events, 34.5 us)
Async XLA Ops:
  7.2 154.1 %all-reduce.5.cloned.1.call-start = ((), (), s32[]{:S(2)}) async-start(), calls=%async_computation | async-start | bytes 1966080 | tf_op jit(solution)/shard_map/psum | solution.py:26
  14.1 1.4 copy-start.7
  161.3 3.3 copy-start
  164.6 0.8 copy-start.1
  266.2 4.4 %copy-start.6 = (f32[1,3,128,128]{2,3,1,0:T(8,128)}, f32[1,3,128,128]{2,3,1,0:T(8,128)S(1)}, u32[]{:S(2)}) copy-start(f32[1,3,128,128]{2,3,1,0:T(8,128)S(1)} %custom-call.46) | copy-start | bytes 589828
  271.0 0.6 copy-start.2
  274.3 0.7 copy-start.4
  290.7 2.2 copy-start.3
  295.7 11.6 %copy-start.5 = (f32[1,256,256]{2,1,0:T(8,128)S(1)}, f32[1,256,256]{2,1,0:T(8,128)}, u32[]{:S(2)}) copy-start(f32[1,256,256]{2,1,0:T(8,128)} %copy-done.4) | copy-start | bytes 786436
Sparse Core Ops, SparseCore 0:
  16.9 144.3 all-reduce.4
where the time goes:
time: 365 us; the launch traced here: 361 us
  other arithmetic  148 us (41%)
  waiting for transfers between devices  144 us (39%)
  local copies, waits for them, and re-layouts  26.2 us (7%)
  matrix products  24.6 us (7%)
  between operations  18 us (5%)
    psum x1, waiting for transfers between devices, on_device(): gram, yskel = lax.psum((gram_local, picked), 'row')  144 us
    another operation x10, other arithmetic, on_device(): lower = jnp.linalg.cholesky(gram / total_rows)  56.4 us
    another operation x7, other arithmetic, on_device(): lower_small = jnp.linalg.cholesky(small)  36.2 us
    another operation x3, other arithmetic, lower_solve(): return jax.scipy.linalg.solve_triangular(lower, right, lower=True)  30.8 us
    another operation x4, other arithmetic, upper_solve(): jax.scipy.linalg.solve_triangular(lower, right, lower=True, trans='T')  20.8 us
    another operation x15, local copies, waits for them, and re-layouts  13 us
    another operation x13, matrix products, lower_solve(): return jax.scipy.linalg.solve_triangular(lower, right, lower=True)  12.5 us
  transfers between devices with their start and end apart: 1, of which 1 were waited for; matrix products, arithmetic and copies ran while one was open for 0% of the time, Pallas kernels for 0%

commit v1 on v0

v1 whole, which is shorter than its diff:
```python
import functools

import jax
import jax.numpy as jnp
from jax import lax
from jax.experimental import pallas as pl
from jax.experimental.pallas import tpu as pltpu
from jax.sharding import PartitionSpec as P

F32, BF16 = jnp.float32, jnp.bfloat16
BLOCK = 128
PANEL = 8
VMEM = pltpu.VMEM


def split(x):
    high = x.astype(BF16).astype(F32)
    rest = x - high
    mid = rest.astype(BF16).astype(F32)
    return high, mid, rest - mid


def pair(x):
    high = x.astype(BF16)
    return high, (x - high.astype(F32)).astype(BF16)


def mul(a, b, dims, exact=True):
    return lax.dot_general(
        a, b, (dims, ((), ())),
        precision=lax.Precision.HIGHEST if exact else None,
        preferred_element_type=F32,
    )


NN, NT, TN = ((1,), (0,)), ((1,), (1,)), ((0,), (0,))


def row(x, k):
    return jnp.broadcast_to(x[k:k + 1], x.shape)


def take(x, index):
    return jnp.take_along_axis(x, index, axis=1)


def identity():
    r = lax.broadcasted_iota(jnp.int32, (BLOCK, BLOCK), 0)
    c = lax.broadcasted_iota(jnp.int32, (BLOCK, BLOCK), 1)
    return jnp.where(r == c, 1.0, 0.0).astype(F32)


def invert_block(work, inverse):
    sub = lax.broadcasted_iota(jnp.int32, (PANEL, BLOCK), 0)
    lane = lax.broadcasted_iota(jnp.int32, (PANEL, BLOCK), 1)

    def panel(p, carry):
        here_a, here_e, last_a, last_e = carry
        base = pl.multiple_of(PANEL * p, PANEL)
        at = sub + base
        after = (at + PANEL) & (BLOCK - 1)
        left = split(jnp.where(lane >= base + 2 * PANEL, last_a, 0.0))
        right = split(jnp.concatenate([last_a, last_e], axis=1))
        lhs = jnp.concatenate([left[i] for i in (0, 0, 1, 0, 1, 2)], axis=0).astype(BF16)
        rhs = jnp.concatenate([right[i] for i in (0, 1, 0, 2, 1, 0)], axis=0).astype(BF16)
        next_a = work[pl.ds(base + PANEL, PANEL), :BLOCK]
        next_e = work[pl.ds(base + PANEL, PANEL), BLOCK:]
        work[:BLOCK, :] = work[:BLOCK, :] - mul(lhs, rhs, TN, exact=False)
        for k in range(PANEL):
            coef = take(row(last_a, k), after)
            next_a = next_a - coef * row(last_a, k)
            next_e = next_e - coef * row(last_e, k)
        own = [take(row(here_a, k), at) for k in range(PANEL)]
        down = [take(row(here_a, k), after) for k in range(PANEL)]
        for k in range(PANEL):
            scale = lax.rsqrt(row(own[k], k))
            lo, ln = own[k] * scale, down[k] * scale
            for m in range(k + 1, PANEL):
                s = row(lo, m)
                own[m] = own[m] - lo * s
                down[m] = down[m] - ln * s
            ua, ue = row(here_a, k) * scale, row(here_e, k) * scale
            below = jnp.where(sub > k, lo, 0.0)
            here_a = jnp.where(sub == k, ua, here_a - below * ua)
            here_e = jnp.where(sub == k, ue, here_e - below * ue)
            next_a = next_a - ln * ua
            next_e = next_e - ln * ue
        inverse[pl.ds(base, PANEL), :] = here_e
        return next_a, next_e, here_a, here_e

    zero = jnp.zeros((PANEL, BLOCK), F32)
    first = (work[:PANEL, :BLOCK], work[:PANEL, BLOCK:], zero, zero)
    lax.fori_loop(0, BLOCK // PANEL, panel, first, unroll=4)


def eliminate(both, n, work, inverse):
    half = n * BLOCK
    work[BLOCK:, :] = jnp.zeros((PANEL, 2 * BLOCK), F32)
    for j in range(n):
        rows = pl.ds(j * BLOCK, BLOCK)
        work[:BLOCK, :BLOCK] = both[rows, j * BLOCK:(j + 1) * BLOCK]
        work[:BLOCK, BLOCK:] = identity()
        invert_block(work, inverse)
        w = inverse[...]
        first, end = (j + 1) * BLOCK, half + j * BLOCK
        both[rows, first:end] = mul(w, both[rows, first:end], NN)
        both[rows, end:end + BLOCK] = w
        for i in range(j + 1, n):
            lead = both[rows, i * BLOCK:(i + 1) * BLOCK]
            below = pl.ds(i * BLOCK, BLOCK)
            span = slice(i * BLOCK, end + BLOCK)
            both[below, span] = both[below, span] - mul(lead, both[rows, span], TN)


def finish(rows_total, sums_ref, xp_ref, q_ref, interp_ref, big, little, work, inverse):
    cols = xp_ref.shape[1]
    n, m = cols // BLOCK, (sums_ref.shape[1] // PANEL - 6) // (cols // BLOCK)
    grab = lambda b: sums_ref[:, b * PANEL:(b + 1) * PANEL, :].reshape(BLOCK, BLOCK)
    big[...] = jnp.zeros_like(big)
    b = 0
    for i in range(n):
        for j in range(i, n):
            big[i * BLOCK:(i + 1) * BLOCK, j * BLOCK:(j + 1) * BLOCK] = grab(b) * (1.0 / rows_total)
            b += 1
    eliminate(big, n, work, inverse)
    e = big[:, cols:]
    yskel = jnp.concatenate(
        [jnp.concatenate([grab(b + i * n + j) for j in range(n)], axis=1) for i in range(m)], axis=0
    )
    qskel = mul(yskel, e, NT)
    little[:, m * BLOCK:] = jnp.zeros((m * BLOCK, m * BLOCK), F32)
    little[:, :m * BLOCK] = mul(qskel, qskel, NT)
    eliminate(little, m, work, inverse)
    w = little[:, m * BLOCK:]
    right = mul(w, mul(w, qskel, NN), TN)
    e_high, e_low = pair(e)
    r_high, r_low = pair(right)

    @pl.loop(0, xp_ref.shape[0] // 256)
    def _(step):
        rows = pl.ds(pl.multiple_of(step * 256, 256), 256)
        x = xp_ref[rows, :]
        q = mul(x, e_high, NT, False) + mul(x, e_low, NT, False)
        q_ref[rows, :] = q
        q_high, q_low = pair(q)
        out = mul(q_high, r_high, NT, False) + mul(q_low, r_high, NT, False) + mul(q_high, r_low, NT, False)
        interp_ref[rows, :] = out.astype(BF16)


def exchange(count, samples_ref, order_ref, skel_ref, sums_ref, xp_ref,
             mine, inbox, total, out_sem, in_sem, out_sem2, in_sem2):
    me = lax.axis_index("row")
    rows, cols = samples_ref.shape
    barrier = pltpu.get_barrier_semaphore()
    for s in range(1, count):
        pl.semaphore_signal(
            barrier, inc=1, device_id={"row": lax.rem(me + s, count)}, device_id_type=pl.DeviceIdType.MESH)
    place = lax.broadcasted_iota(jnp.int32, (cols, cols), 0)
    move = jnp.where(place == order_ref[...], 1.0, 0.0).astype(BF16)
    xp_ref[...] = mul(samples_ref[...], move, NN, False).astype(BF16)
    keys = skel_ref.shape[1]
    at = lax.broadcasted_iota(jnp.int32, (rows, keys), 0) + me * rows
    pick = jnp.where(at == skel_ref[...], 1.0, 0.0).astype(BF16)
    xp = xp_ref[...]
    n = cols // BLOCK

    def put(b, value):
        mine[:, b * PANEL:(b + 1) * PANEL, :] = value.reshape(count, PANEL, BLOCK)

    b = 0
    for i in range(n):
        part = mul(xp[:, i * BLOCK:(i + 1) * BLOCK], xp[:, i * BLOCK:], TN, False)
        for j in range(i, n):
            put(b, part[:, (j - i) * BLOCK:(j - i + 1) * BLOCK])
            b += 1
    chosen = mul(pick, xp, TN, False)
    for i in range(keys // BLOCK):
        for j in range(n):
            put(b, chosen[i * BLOCK:(i + 1) * BLOCK, j * BLOCK:(j + 1) * BLOCK])
            b += 1
    pl.semaphore_wait(barrier, count - 1)
    steps = sorted(range(1, count), key=lambda s: -min(s, count - s))

    def send(source, target, s, a, b):
        return pltpu.make_async_remote_copy(
            src_ref=source, dst_ref=target, send_sem=a.at[s], recv_sem=b.at[s],
            device_id={"row": lax.rem(me + s, count)}, device_id_type=pl.DeviceIdType.MESH)

    scatter = {s: send(mine.at[lax.rem(me + s, count)], inbox.at[s], s, out_sem, in_sem) for s in steps}
    for s in steps:
        scatter[s].start()
    acc = mine[me]
    for s in reversed(steps):
        scatter[s].wait_recv()
        acc = acc + inbox[s]
    total[me] = acc
    gather = {s: send(total.at[me], total.at[me], s, out_sem2, in_sem2) for s in steps}
    for s in steps:
        gather[s].start()
    for s in steps:
        scatter[s].wait_send()
    for s in reversed(steps):
        gather[s].wait_send()
        gather[s].wait_recv()
    sums_ref[...] = total[...]


def on_device(count, samples, column_order, skeleton):
    _, rows, cols = samples.shape
    keys = skeleton.shape[1]
    n, m = cols // BLOCK, keys // BLOCK
    depth = (n * (n + 1) // 2 + m * n) * PANEL
    whole = pl.BlockSpec(memory_space=VMEM)
    sums, permuted = pl.pallas_call(
        functools.partial(exchange, count),
        out_shape=(jax.ShapeDtypeStruct((count, depth, BLOCK), F32), jax.ShapeDtypeStruct((rows, cols), BF16)),
        in_specs=[whole] * 3,
        out_specs=(whole, whole),
        scratch_shapes=[VMEM((count, depth, BLOCK), F32)] * 3 + [pltpu.SemaphoreType.DMA((count,))] * 4,
        compiler_params=pltpu.CompilerParams(collective_id=0, has_side_effects=True),
    )(samples[0], column_order, skeleton)
    q_factor, interp = pl.pallas_call(
        functools.partial(finish, rows * count),
        out_shape=(jax.ShapeDtypeStruct((rows, cols), F32), jax.ShapeDtypeStruct((rows, keys), BF16)),
        in_specs=[whole] * 2,
        out_specs=(whole, whole),
        scratch_shapes=[
            VMEM((cols, 2 * cols), F32), VMEM((keys, 2 * keys), F32),
            VMEM((BLOCK + PANEL, 2 * BLOCK), F32), VMEM((BLOCK, BLOCK), F32),
        ],
    )(sums, permuted)
    return q_factor[None], interp[None]


def solution(mesh):
    placed = (P("node", "row", None), P("node", None), P("node", None))
    return jax.shard_map(
        functools.partial(on_device, mesh.shape["row"]),
        mesh=mesh,
        in_specs=placed,
        out_specs=(P("node", "row", None), P("node", "row", None)),
        check_vma=False,
    )
```

time: 365 us -> 116 us (0.32)
  other arithmetic: 148 us -> 0 us
  waiting for transfers between devices: 144 us -> 0 us
  Pallas kernels: 0 us -> 114 us
  local copies, waits for them, and re-layouts: 26.2 us -> 0 us
  matrix products: 24.6 us -> 0 us
  between operations: 18 us -> 0.64 us
    psum x1 -> x0, waiting for transfers between devices: 144 us -> none  [on_device(): gram, yskel = lax.psum((gram_local, picked), 'row')]
    another operation x24 -> x0, other arithmetic: 144 us -> none  [the longest x10 56.4 us: on_device(): lower = jnp.linalg.cholesky(gram / total_rows)]
    pallas_call x0 -> x2, Pallas kernels: none -> 114 us  [the longest x1 88.5 us: on_device(): pl.pallas_call(functools.partial(exchange, count), out_shape=(jax.ShapeDt...]
    another operation x22 -> x0, matrix products: 18.4 us -> none  [the longest x13 12.5 us: lower_solve(): return jax.scipy.linalg.solve_triangular(lower, right, lower=True)]
    another operation x22 -> x0, local copies, waits for them, and re-layouts: 13.2 us -> none
    dot_general x4 -> x0, matrix products: 6.22 us -> none  [the longest x1 2.73 us: on_device(): jnp.einsum('frc,fkc->frk', q_factor, qskel, precision=lax.Precision.HIGHEST)]
    unnamed x19 -> x0, local copies, waits for them, and re-layouts: 6.19 us -> none
    gather x2 -> x0, local copies, waits for them, and re-layouts: 4.74 us -> none  [on_device(): block[:, order]]
  transfers between devices with their start and end apart: 1 -> 0, of which waited for: 1 -> 0; matrix products, arithmetic and copies ran while one was open for 0% -> 0% of each run, Pallas kernels for 0% -> 0%
where the time goes in v1:
time: 116 us; the launch traced here: 115 us
  Pallas kernels  114 us (98%)
    pallas_call x1, Pallas kernels, on_device(): pl.pallas_call(functools.partial(exchange, count), out_shape=(jax.ShapeDt...  88.5 us
    pallas_call x1, Pallas kernels, on_device(): pl.pallas_call(functools.partial(finish, rows * count), out_shape=(jax.Sh...  25.4 us

profile of v1, /device:TPU:6, one launch (start us, length us, event | category | flops | bytes accessed | tf_op | source)
XLA Modules:
  0.0 114.5 jit_solution(15965027259989209324)
XLA Ops:
  0.6 88.5 %shard_map.50 = (f32[16,96,128]{2,1,0:T(8,128)}, bf16[1024,384]{1,0:T(8,128)(2,1)}) custom-call(bf16[1024,384]{1,0:T(8,128)(2,1)} %bitcast.3, s32[1,384]{1,0:T(1,128)} %order_ref.1, s32[1,256]{1,0:T(1,128)} %skel_ref.1), custom_call_target="tpu_custom_call" | custom-call | tf_op jit(solution)/shard_map/pallas_call | solution.py:214
  89.1 25.4 %shard_map.51 = (f32[1024,384]{1,0:T(8,128)}, bf16[1024,256]{1,0:T(8,128)(2,1)}) custom-call(f32[16,96,128]{2,1,0:T(8,128)} %get-tuple-element.6.sums_ref, bf16[1024,384]{1,0:T(8,128)(2,1)} %get-tuple-element.7.xp_ref), custom_call_target="tpu_custom_call" | custom-call | tf_op jit(solution)/shard_map/pallas_call | solution.py:222

commit v2 on v1

v2 whole, which is shorter than its diff:
```python
import jax
import jax.numpy as jnp
from jax import lax
from jax.experimental import pallas as pl
from jax.experimental.pallas import tpu as pltpu
from jax.sharding import PartitionSpec as P

F32, BF16 = jnp.float32, jnp.bfloat16
BLOCK = 128
PANEL = 8
RING = 16
VMEM = pltpu.VMEM


def split(x):
    high = x.astype(BF16).astype(F32)
    rest = x - high
    mid = rest.astype(BF16).astype(F32)
    return high, mid, rest - mid


def pair(x):
    high = x.astype(BF16)
    return high, (x - high.astype(F32)).astype(BF16)


def mul(a, b, dims, exact=True):
    return lax.dot_general(
        a, b, (dims, ((), ())),
        precision=lax.Precision.HIGHEST if exact else None,
        preferred_element_type=F32,
    )


NN, NT, TN = ((1,), (0,)), ((1,), (1,)), ((0,), (0,))


def row(x, k):
    return jnp.broadcast_to(x[k:k + 1], x.shape)


def take(x, index):
    return jnp.take_along_axis(x, index, axis=1)


def identity():
    r = lax.broadcasted_iota(jnp.int32, (BLOCK, BLOCK), 0)
    c = lax.broadcasted_iota(jnp.int32, (BLOCK, BLOCK), 1)
    return jnp.where(r == c, 1.0, 0.0).astype(F32)


def invert_block(work, inverse):
    sub = lax.broadcasted_iota(jnp.int32, (PANEL, BLOCK), 0)
    lane = lax.broadcasted_iota(jnp.int32, (PANEL, BLOCK), 1)

    def panel(p, carry):
        here_a, here_e, last_a, last_e = carry
        base = pl.multiple_of(PANEL * p, PANEL)
        at = sub + base
        after = (at + PANEL) & (BLOCK - 1)
        left = split(jnp.where(lane >= base + 2 * PANEL, last_a, 0.0))
        right = split(jnp.concatenate([last_a, last_e], axis=1))
        lhs = jnp.concatenate([left[i] for i in (0, 0, 1, 0, 1, 2)], axis=0).astype(BF16)
        rhs = jnp.concatenate([right[i] for i in (0, 1, 0, 2, 1, 0)], axis=0).astype(BF16)
        next_a = work[pl.ds(base + PANEL, PANEL), :BLOCK]
        next_e = work[pl.ds(base + PANEL, PANEL), BLOCK:]
        work[:BLOCK, :] = work[:BLOCK, :] - mul(lhs, rhs, TN, exact=False)
        for k in range(PANEL):
            coef = take(row(last_a, k), after)
            next_a = next_a - coef * row(last_a, k)
            next_e = next_e - coef * row(last_e, k)
        own = [take(row(here_a, k), at) for k in range(PANEL)]
        down = [take(row(here_a, k), after) for k in range(PANEL)]
        for k in range(PANEL):
            scale = lax.rsqrt(row(own[k], k))
            lo, ln = own[k] * scale, down[k] * scale
            for m in range(k + 1, PANEL):
                s = row(lo, m)
                own[m] = own[m] - lo * s
                down[m] = down[m] - ln * s
            ua, ue = row(here_a, k) * scale, row(here_e, k) * scale
            below = jnp.where(sub > k, lo, 0.0)
            here_a = jnp.where(sub == k, ua, here_a - below * ua)
            here_e = jnp.where(sub == k, ue, here_e - below * ue)
            next_a = next_a - ln * ua
            next_e = next_e - ln * ue
        inverse[pl.ds(base, PANEL), :] = here_e
        return next_a, next_e, here_a, here_e

    zero = jnp.zeros((PANEL, BLOCK), F32)
    first = (work[:PANEL, :BLOCK], work[:PANEL, BLOCK:], zero, zero)
    lax.fori_loop(0, BLOCK // PANEL, panel, first, unroll=4)


def eliminate(both, n, work, inverse, between=None):
    half = n * BLOCK
    work[BLOCK:, :] = jnp.zeros((PANEL, 2 * BLOCK), F32)
    for j in range(n):
        rows = pl.ds(j * BLOCK, BLOCK)
        work[:BLOCK, :BLOCK] = both[rows, j * BLOCK:(j + 1) * BLOCK]
        work[:BLOCK, BLOCK:] = identity()
        invert_block(work, inverse)
        if between is not None and j == 0:
            between()
        w = inverse[...]
        first, end = (j + 1) * BLOCK, half + j * BLOCK
        both[rows, first:end] = mul(w, both[rows, first:end], NN)
        both[rows, end:end + BLOCK] = w
        for i in range(j + 1, n):
            lead = both[rows, i * BLOCK:(i + 1) * BLOCK]
            below = pl.ds(i * BLOCK, BLOCK)
            span = slice(i * BLOCK, end + BLOCK)
            both[below, span] = both[below, span] - mul(lead, both[rows, span], TN)


def finish(e_ref, yskel_ref, xp_ref, q_ref, interp_ref, little, work, inverse):
    keys = yskel_ref.shape[0]
    e = e_ref[...]
    qskel = mul(yskel_ref[...], e, NT)
    little[:, keys:] = jnp.zeros((keys, keys), F32)
    little[:, :keys] = mul(qskel, qskel, NT)
    eliminate(little, keys // BLOCK, work, inverse)
    w = little[:, keys:]
    right = mul(w, mul(w, qskel, NN), TN)
    e_high, e_low = pair(e)
    r_high, r_low = pair(right)

    @pl.loop(0, xp_ref.shape[0] // 256)
    def _(step):
        rows = pl.ds(pl.multiple_of(step * 256, 256), 256)
        x = xp_ref[rows, :]
        q = mul(x, e_high, NT, False) + mul(x, e_low, NT, False)
        q_ref[rows, :] = q
        q_high, q_low = pair(q)
        out = mul(q_high, r_high, NT, False) + mul(q_low, r_high, NT, False) + mul(q_high, r_low, NT, False)
        interp_ref[rows, :] = out.astype(BF16)


def places():
    r = lax.broadcasted_iota(jnp.int32, (BLOCK, BLOCK), 0)
    c = lax.broadcasted_iota(jnp.int32, (BLOCK, BLOCK), 1)
    return r, c


def fold(first, second, third):
    r, c = places()
    edge = jnp.sum(jnp.where(r == c, first, 0.0), axis=0, keepdims=True)
    corner = first[BLOCK - 1:, BLOCK - 1:]
    one = jnp.where(r > c, first, second)
    two = jnp.where(r == c + 1, edge, third)
    return one, jnp.where((r == BLOCK - 1) & (c == 0), corner, two)


def unfold(one, two):
    r, c = places()
    edge = jnp.sum(jnp.where(r == c + 1, two, 0.0), axis=0, keepdims=True)
    corner = two[BLOCK - 1:, :1]
    edge = jnp.where(c == BLOCK - 1, corner, edge)
    first = jnp.where(r < c, one.T, jnp.where(r == c, edge, 0.0))
    return first, jnp.where(r <= c, one, 0.0), jnp.where(r <= c, two, 0.0)


def exchange(samples_ref, order_ref, skel_ref, e_ref, yskel_ref, xp_ref,
             gmine, gnear, gedge, gpart, gmate, gfull,
             ymine, ynear, yedge, ypart, ymate, yfull,
             big, work, inverse, out_sem, in_sem):
    me = lax.axis_index("row")
    rows, cols = samples_ref.shape
    keys = skel_ref.shape[1]
    n, m = cols // BLOCK, keys // BLOCK
    around = lambda d, size: lax.rem(me + (d + RING), size)
    barrier = pltpu.get_barrier_semaphore()
    near = (3, -3, 2, -2, 1, -1)
    partners = (8, 4, -4) + near
    for d in partners:
        pl.semaphore_signal(
            barrier, inc=1, device_id={"row": around(d, RING)}, device_id_type=pl.DeviceIdType.MESH)
    number = iter(range(32))

    def send(source, target, d):
        i = next(number)
        copy = pltpu.make_async_remote_copy(
            src_ref=source, dst_ref=target, send_sem=out_sem.at[i], recv_sem=in_sem.at[i],
            device_id={"row": around(d, RING)}, device_id_type=pl.DeviceIdType.MESH)
        copy.start()
        return copy

    place = lax.broadcasted_iota(jnp.int32, (cols, cols), 0)
    move = jnp.where(place == order_ref[...], 1.0, 0.0).astype(BF16)
    xp_ref[...] = mul(samples_ref[...], move, NN, False).astype(BF16)
    xp = xp_ref[...]
    parts = [
        [mul(xp[:, i * BLOCK:(i + 1) * BLOCK], xp[:, i * BLOCK:], TN, False)[:, j * BLOCK:(j + 1) * BLOCK]
         for j in range(n - i)] for i in range(n)
    ]
    folded = fold(*[parts[i][0] for i in range(n)]) + (parts[0][1], parts[0][2], parts[1][1])
    for b, value in enumerate(folded):
        gmine[:, b * 16:(b + 1) * 16, :] = value.reshape(8, 16, BLOCK)
    pl.semaphore_wait(barrier, len(partners))

    sent = []
    unit = around(0, 8)
    ghalf = gmine.shape[1] // 2
    ends = ((4, 0), (-4, 1))
    here = [send(gmine.at[around(4, 8), pl.ds(h * ghalf, ghalf)], gedge.at[h], d) for d, h in ends]
    here += [send(gmine.at[around(d, 8)], gnear.at[k], d) for k, d in enumerate(near)]
    sent += here

    at = lax.broadcasted_iota(jnp.int32, (rows, keys), 0) + me * rows
    pick = jnp.where(at == skel_ref[...], 1.0, 0.0).astype(BF16)
    chosen = mul(pick, xp, TN, False)
    for b in range(m * n):
        i, j = b // n, b % n
        value = chosen[i * BLOCK:(i + 1) * BLOCK, j * BLOCK:(j + 1) * BLOCK].reshape(4, 4, PANEL, BLOCK)
        for k in range(4):
            ymine[k, :, b * PANEL:(b + 1) * PANEL, :] = value[:, k]
    residue, quarter = around(0, 4), lax.div(me, 4)
    yhalf = ymine.shape[2] // 2
    pairs = ((2, 0), (-2, 1))
    there = [send(ymine.at[around(2, 4), :, pl.ds(h * yhalf, yhalf)], yedge.at[h], d) for d, h in pairs]
    there += [send(ymine.at[around(d, 4)], ynear.at[k], d) for k, d in enumerate((1, -1))]
    sent += there

    for copy in here:
        copy.wait_recv()
    acc = gmine[unit] + jnp.concatenate([gedge[0], gedge[1]], axis=0)
    for k in range(len(near)):
        acc = acc + gnear[k]
    gpart[...] = acc
    across = send(gpart, gmate, 8)
    sent.append(across)

    for copy in there:
        copy.wait_recv()
    ypart[...] = ymine[residue] + ynear[0] + ynear[1] + jnp.concatenate([yedge[0], yedge[1]], axis=1)
    far = (8, 4, -4)
    there = [send(ypart.at[lax.rem(quarter + (d // 4 + 4), 4)], ymate.at[k], d) for k, d in enumerate(far)]
    sent += there

    across.wait_recv()
    gfull[unit] = gpart[...] + gmate[...]
    here = []
    for d, h in ends:
        piece = gfull.at[unit, pl.ds(h * ghalf, ghalf)]
        here.append(send(piece, piece, d))
    here += [send(gfull.at[unit], gfull.at[unit], d) for d in near]
    sent += here

    for copy in there:
        copy.wait_recv()
    yfull[residue, quarter] = ypart[quarter] + ymate[0] + ymate[1] + ymate[2]
    there = [send(yfull.at[residue, quarter], yfull.at[residue, quarter], d) for d in far]
    sent += there

    for copy in here:
        copy.wait_recv()
    scale = 1.0 / (rows * RING)
    full = [gfull[:, b * 16:(b + 1) * 16, :].reshape(BLOCK, BLOCK) * scale for b in range(len(folded))]
    big[...] = jnp.zeros_like(big)
    for i, value in enumerate(unfold(full[0], full[1])):
        big[i * BLOCK:(i + 1) * BLOCK, i * BLOCK:(i + 1) * BLOCK] = value
    for (i, j), value in zip(((0, 1), (0, 2), (1, 2)), full[2:]):
        big[i * BLOCK:(i + 1) * BLOCK, j * BLOCK:(j + 1) * BLOCK] = value

    last = []

    def hand_on():
        for copy in there:
            copy.wait_recv()
        for d, h in pairs:
            piece = yfull.at[residue, :, pl.ds(h * yhalf, yhalf)]
            last.append(send(piece, piece, d))
        for d in (1, -1):
            last.append(send(yfull.at[residue], yfull.at[residue], d))

    eliminate(big, n, work, inverse, hand_on)
    e_ref[...] = big[:, cols:]
    for copy in last:
        copy.wait_recv()
    for b in range(m * n):
        i, j = b // n, b % n
        value = jnp.stack([yfull[k, :, b * PANEL:(b + 1) * PANEL, :] for k in range(4)], axis=1)
        yskel_ref[i * BLOCK:(i + 1) * BLOCK, j * BLOCK:(j + 1) * BLOCK] = value.reshape(BLOCK, BLOCK)
    for copy in sent + last:
        copy.wait_send()


def on_device(samples, column_order, skeleton):
    _, rows, cols = samples.shape
    keys = skeleton.shape[1]
    n, m = cols // BLOCK, keys // BLOCK
    whole = pl.BlockSpec(memory_space=VMEM)
    deep, tall = 5 * 16, m * n * PANEL
    room = [VMEM((BLOCK + PANEL, 2 * BLOCK), F32), VMEM((BLOCK, BLOCK), F32)]
    e, yskel, permuted = pl.pallas_call(
        exchange,
        out_shape=(
            jax.ShapeDtypeStruct((cols, cols), F32), jax.ShapeDtypeStruct((keys, cols), F32),
            jax.ShapeDtypeStruct((rows, cols), BF16),
        ),
        in_specs=[whole] * 3,
        out_specs=(whole,) * 3,
        scratch_shapes=[
            VMEM((8, deep, BLOCK), F32), VMEM((6, deep, BLOCK), F32), VMEM((2, deep // 2, BLOCK), F32),
            VMEM((deep, BLOCK), F32), VMEM((deep, BLOCK), F32), VMEM((8, deep, BLOCK), F32),
            VMEM((4, 4, tall, BLOCK), F32), VMEM((2, 4, tall, BLOCK), F32), VMEM((2, 4, tall // 2, BLOCK), F32),
            VMEM((4, tall, BLOCK), F32), VMEM((3, tall, BLOCK), F32), VMEM((4, 4, tall, BLOCK), F32),
            VMEM((cols, 2 * cols), F32),
        ] + room + [pltpu.SemaphoreType.DMA((32,))] * 2,
        compiler_params=pltpu.CompilerParams(collective_id=0, has_side_effects=True),
    )(samples[0], column_order, skeleton)
    q_factor, interp = pl.pallas_call(
        finish,
        out_shape=(jax.ShapeDtypeStruct((rows, cols), F32), jax.ShapeDtypeStruct((rows, keys), BF16)),
        in_specs=[whole] * 3,
        out_specs=(whole, whole),
        scratch_shapes=[VMEM((keys, 2 * keys), F32)] + room,
    )(e, yskel, permuted)
    return q_factor[None], interp[None]


def solution(mesh):
    placed = (P("node", "row", None), P("node", None), P("node", None))
    return jax.shard_map(
        on_device,
        mesh=mesh,
        in_specs=placed,
        out_specs=(P("node", "row", None), P("node", "row", None)),
        check_vma=False,
    )
```

time: 116 us -> 75.6 us (0.65); the launches traced: 115 us -> 75.5 us
  Pallas kernels: 114 us -> 74.8 us
    pallas_call x2, Pallas kernels: 114 us -> 74.8 us  [the longest x1 59.4 us: on_device(): pl.pallas_call(exchange, out_shape=(jax.ShapeDtypeStruct((cols, cols), F3...]
where the time goes in v2:
time: 75.6 us; the launch traced here: 75.5 us
  Pallas kernels  74.8 us (99%)
    pallas_call x1, Pallas kernels, on_device(): pl.pallas_call(exchange, out_shape=(jax.ShapeDtypeStruct((cols, cols), F3...  59.4 us
    pallas_call x1, Pallas kernels, on_device(): pl.pallas_call(finish, out_shape=(jax.ShapeDtypeStruct((rows, cols), F32)...  15.5 us

profile of v2, /device:TPU:6, one launch (start us, length us, event | category | flops | bytes accessed | tf_op | source)
XLA Modules:
  0.0 75.5 jit_solution(4431138158116412195)
XLA Ops:
  0.6 59.4 %shard_map.50 = (f32[384,384]{1,0:T(8,128)}, f32[256,384]{1,0:T(8,128)}, bf16[1024,384]{1,0:T(8,128)(2,1)}) custom-call(bf16[1024,384]{1,0:T(8,128)(2,1)} %bitcast.3, s32[1,384]{1,0:T(1,128)} %order_ref.1, s32[1,256]{1,0:T(1,128)} %skel_ref.1), custom_call_target="tpu_custom_call" | custom-call | tf_op jit(solution)/shard_map/pallas_call | solution.py:295
  60.0 15.5 %shard_map.51 = (f32[1024,384]{1,0:T(8,128)}, bf16[1024,256]{1,0:T(8,128)(2,1)}) custom-call(f32[384,384]{1,0:T(8,128)} %get-tuple-element.7.e_ref, f32[256,384]{1,0:T(8,128)} %get-tuple-element.8.yskel_ref, bf16[1024,384]{1,0:T(8,128)(2,1)} %get-tuple-element.9.xp_ref), custom_call_target="tpu_custom_call" | custom-call | tf_op jit(solution)/shard_map/pallas_call | solution.py:312

commit v3 on v2

v3 whole, which is shorter than its diff:
```python
import functools

import jax
import jax.numpy as jnp
from jax import lax
from jax.experimental import pallas as pl
from jax.experimental.pallas import tpu as pltpu
from jax.sharding import PartitionSpec as P

F32, BF16 = jnp.float32, jnp.bfloat16
BLOCK = 128
PANEL = 8
RING = 16
VMEM = pltpu.VMEM


def split(x):
    high = x.astype(BF16).astype(F32)
    rest = x - high
    mid = rest.astype(BF16).astype(F32)
    return high, mid, rest - mid


def pair(x):
    high = x.astype(BF16)
    return high, (x - high.astype(F32)).astype(BF16)


def mul(a, b, dims, exact=True):
    return lax.dot_general(
        a, b, (dims, ((), ())),
        precision=lax.Precision.HIGHEST if exact else None,
        preferred_element_type=F32,
    )


NN, NT, TN = ((1,), (0,)), ((1,), (1,)), ((0,), (0,))


def row(x, k):
    return jnp.broadcast_to(x[k:k + 1], x.shape)


def take(x, index):
    return jnp.take_along_axis(x, index, axis=1)


def identity():
    r = lax.broadcasted_iota(jnp.int32, (BLOCK, BLOCK), 0)
    c = lax.broadcasted_iota(jnp.int32, (BLOCK, BLOCK), 1)
    return jnp.where(r == c, 1.0, 0.0).astype(F32)


def invert_block(work, inverse, beside=None):
    sub = lax.broadcasted_iota(jnp.int32, (PANEL, BLOCK), 0)
    lane = lax.broadcasted_iota(jnp.int32, (PANEL, BLOCK), 1)

    def panel(p, carry):
        here_a, here_e, last_a, last_e = carry
        base = pl.multiple_of(PANEL * p, PANEL)
        at = sub + base
        after = (at + PANEL) & (BLOCK - 1)
        left = split(jnp.where(lane >= base + 2 * PANEL, last_a, 0.0))
        right = split(jnp.concatenate([last_a, last_e], axis=1))
        lhs = jnp.concatenate([left[i] for i in (0, 0, 1, 0, 1, 2)], axis=0).astype(BF16)
        rhs = jnp.concatenate([right[i] for i in (0, 1, 0, 2, 1, 0)], axis=0).astype(BF16)
        next_a = work[pl.ds(base + PANEL, PANEL), :BLOCK]
        next_e = work[pl.ds(base + PANEL, PANEL), BLOCK:]
        work[:BLOCK, :] = work[:BLOCK, :] - mul(lhs, rhs, TN, exact=False)
        for k in range(PANEL):
            coef = take(row(last_a, k), after)
            next_a = next_a - coef * row(last_a, k)
            next_e = next_e - coef * row(last_e, k)
        own = [take(row(here_a, k), at) for k in range(PANEL)]
        down = [take(row(here_a, k), after) for k in range(PANEL)]
        for k in range(PANEL):
            scale = lax.rsqrt(row(own[k], k))
            lo, ln = own[k] * scale, down[k] * scale
            for m in range(k + 1, PANEL):
                s = row(lo, m)
                own[m] = own[m] - lo * s
                down[m] = down[m] - ln * s
            ua, ue = row(here_a, k) * scale, row(here_e, k) * scale
            below = jnp.where(sub > k, lo, 0.0)
            here_a = jnp.where(sub == k, ua, here_a - below * ua)
            here_e = jnp.where(sub == k, ue, here_e - below * ue)
            next_a = next_a - ln * ua
            next_e = next_e - ln * ue
        inverse[pl.ds(base, PANEL), :] = here_e
        return next_a, next_e, here_a, here_e

    def several(step, carry):
        if beside is not None:
            beside(step)
        for k in range(4):
            carry = panel(step * 4 + k, carry)
        return carry

    zero = jnp.zeros((PANEL, BLOCK), F32)
    first = (work[:PANEL, :BLOCK], work[:PANEL, BLOCK:], zero, zero)
    lax.fori_loop(0, BLOCK // PANEL // 4, several, first)


def eliminate(both, n, work, inverse, right=None, between=None, beside=None):
    half = n * BLOCK
    work[BLOCK:, :] = jnp.zeros((PANEL, 2 * BLOCK), F32)
    for j in range(n):
        rows = pl.ds(j * BLOCK, BLOCK)
        work[:BLOCK, :BLOCK] = both[rows, j * BLOCK:(j + 1) * BLOCK]
        work[:BLOCK, BLOCK:] = identity()
        invert_block(work, inverse, functools.partial(beside, j) if beside is not None else None)
        if between is not None:
            between(j)
        w = inverse[...]
        first, end = (j + 1) * BLOCK, half + j * BLOCK
        both[rows, first:end] = mul(w, both[rows, first:end], NN)
        both[rows, end:end + BLOCK] = w
        if right is not None:
            right[rows, :] = mul(w, right[rows, :], NN)
        for i in range(j + 1, n):
            lead = both[rows, i * BLOCK:(i + 1) * BLOCK]
            below = pl.ds(i * BLOCK, BLOCK)
            span = slice(i * BLOCK, end + BLOCK)
            both[below, span] = both[below, span] - mul(lead, both[rows, span], TN)
            if right is not None:
                right[below, :] = right[below, :] - mul(lead, right[rows, :], TN)


def finish(q_ref, high_ref, low_ref, right_ref, q_out, interp_out, interp, sems):
    whole_q = pltpu.make_async_copy(q_ref, q_out, sems.at[0])
    whole_q.start()
    r_high, r_low = pair(right_ref[...])
    size = q_ref.shape[0] // 4
    copies = []
    for step in range(4):
        rows = pl.ds(step * size, size)
        high, low = high_ref[rows, :], low_ref[rows, :]
        out = mul(high, r_high, NT, False) + mul(low, r_high, NT, False) + mul(high, r_low, NT, False)
        interp[rows, :] = out.astype(BF16)
        copies.append(pltpu.make_async_copy(interp.at[rows, :], interp_out.at[rows, :], sems.at[1 + step]))
        copies[-1].start()
    whole_q.wait()
    for copy in copies:
        copy.wait()


def places():
    r = lax.broadcasted_iota(jnp.int32, (BLOCK, BLOCK), 0)
    c = lax.broadcasted_iota(jnp.int32, (BLOCK, BLOCK), 1)
    return r, c


def fold(first, second, third):
    r, c = places()
    edge = jnp.sum(jnp.where(r == c, first, 0.0), axis=0, keepdims=True)
    corner = first[BLOCK - 1:, BLOCK - 1:]
    one = jnp.where(r > c, first, second)
    two = jnp.where(r == c + 1, edge, third)
    return one, jnp.where((r == BLOCK - 1) & (c == 0), corner, two)


def unfold(one, two):
    r, c = places()
    edge = jnp.sum(jnp.where(r == c + 1, two, 0.0), axis=0, keepdims=True)
    corner = two[BLOCK - 1:, :1]
    edge = jnp.where(c == BLOCK - 1, corner, edge)
    first = jnp.where(r < c, one.T, jnp.where(r == c, edge, 0.0))
    return first, jnp.where(r <= c, one, 0.0), jnp.where(r <= c, two, 0.0)


class Stream:
    def __init__(self, me, send, mine, near, edge, part, mate, full):
        self.me, self.send = me, send
        self.mine, self.near, self.edge = mine, near, edge
        self.part, self.mate, self.full = part, mate, full
        self.residue, self.quarter = lax.rem(me, 4), lax.div(me, 4)
        self.sent, self.due = [], []

    def begin(self, copies):
        self.due = copies
        self.sent += copies

    def arrive(self):
        for copy in self.due:
            copy.wait_recv()

    def put(self, b, value):
        value = value.reshape(4, 4, PANEL, BLOCK)
        for k in range(4):
            self.mine[k, :, b * PANEL:(b + 1) * PANEL, :] = value[:, k]

    def get(self, b):
        value = jnp.stack([self.full[k, :, b * PANEL:(b + 1) * PANEL, :] for k in range(4)], axis=1)
        return value.reshape(BLOCK, BLOCK)

    def spread(self):
        self.begin(
            [self.send(self.mine.at[lax.rem(self.me + 2, 4), pl.ds(h, 2)], self.edge.at[pl.ds(h, 2)], d)
             for d, h in ((2, 0), (-2, 2))]
            + [self.send(self.mine.at[lax.rem(self.me + d + RING, 4)], self.near.at[k], d)
               for k, d in enumerate((1, -1))])

    def reduce_near(self):
        self.arrive()
        self.part[...] = (self.mine[self.residue] + self.edge[...]) + (self.near[0] + self.near[1])
        self.begin([self.send(self.part.at[lax.rem(self.quarter + (d // 4 + 4), 4)], self.mate.at[k], d)
                    for k, d in enumerate((8, 4, -4))])

    def reduce_far(self):
        self.arrive()
        own = self.full.at[self.residue, self.quarter]
        own[...] = (self.part[self.quarter] + self.mate[0]) + (self.mate[1] + self.mate[2])
        self.begin([self.send(own, own, d) for d in (8, 4, -4)])

    def hand_back(self):
        self.arrive()
        piece = lambda h: self.full.at[self.residue, pl.ds(h, 2)]
        self.begin([self.send(piece(h), piece(h), d) for d, h in ((2, 0), (-2, 2))]
                   + [self.send(self.full.at[self.residue], self.full.at[self.residue], d) for d in (1, -1)])

    def drain(self):
        for copy in self.sent:
            copy.wait_send()


def room_of(blocks):
    rows = blocks * PANEL
    return [VMEM(shape + (rows, BLOCK), F32) for shape in ((4, 4), (2, 4), (4,), (4,), (3,), (4, 4))]


def factor(samples_hbm, order_hbm, skel_hbm, q_ref, high_ref, low_ref, right_ref, *scratch):
    streams = scratch[:24]
    (big, little, solved, samples, xp_ref, order_ref, skel_ref, work, inverse, out_sem, in_sem, load_sem, known) = scratch[24:]
    me = lax.axis_index("row")
    rows, cols = samples.shape
    keys = skel_ref.shape[1]
    n, m = cols // BLOCK, keys // BLOCK
    around = lambda d: lax.rem(me + (d + RING), RING)
    barrier = pltpu.get_barrier_semaphore()
    partners = (2, -2, 1, -1)
    for d in partners:
        pl.semaphore_signal(
            barrier, inc=1, device_id={"row": around(d)}, device_id_type=pl.DeviceIdType.MESH)
    loads = [pltpu.make_async_copy(a, b, load_sem.at[k]) for k, (a, b) in enumerate(
        ((order_hbm, order_ref), (samples_hbm, samples), (skel_hbm, skel_ref)))]
    for load in loads:
        load.start()
    number = iter(range(56))

    def send(source, target, d):
        i = next(number)
        copy = pltpu.make_async_remote_copy(
            src_ref=source, dst_ref=target, send_sem=out_sem.at[i], recv_sem=in_sem.at[i],
            device_id={"row": around(d)}, device_id_type=pl.DeviceIdType.MESH)
        copy.start()
        return copy

    lead, rest, upper, lower = [Stream(me, send, *streams[6 * k:6 * k + 6]) for k in range(4)]
    big[...] = jnp.zeros_like(big)
    loads[0].wait()
    place = lax.broadcasted_iota(jnp.int32, (cols, cols), 0)
    move = jnp.where(place == order_ref[...], 1.0, 0.0).astype(BF16)
    loads[1].wait()
    xp_ref[...] = mul(samples[...], move, NN, False).astype(BF16)
    xp = xp_ref[...]
    parts = [
        [mul(xp[:, i * BLOCK:(i + 1) * BLOCK], xp[:, i * BLOCK:], TN, False)[:, j * BLOCK:(j + 1) * BLOCK]
         for j in range(n - i)] for i in range(n)
    ]
    one, two = fold(parts[1][0], parts[0][0], parts[2][0])
    lead.put(0, one)
    for b, value in enumerate((two, parts[0][1], parts[0][2], parts[1][1])):
        rest.put(b, value)
    pl.semaphore_wait(barrier, len(partners))
    lead.spread()
    rest.spread()

    def tell(k, steps):
        for d in steps:
            pl.semaphore_signal(
                known.at[k], inc=1, device_id={"row": around(d)}, device_id_type=pl.DeviceIdType.MESH)

    tell(0, (2, -2))

    loads[2].wait()
    at = lax.broadcasted_iota(jnp.int32, (rows, keys), 0) + me * rows
    pick = jnp.where(at == skel_ref[...], 1.0, 0.0).astype(BF16)
    chosen = mul(pick, xp, TN, False)
    for half, stream in enumerate((upper, lower)):
        for j in range(n):
            stream.put(j, chosen[half * BLOCK:(half + 1) * BLOCK, j * BLOCK:(j + 1) * BLOCK])
    pl.semaphore_wait(known.at[0], 2)
    tell(1, (4, -4))
    pl.semaphore_wait(known.at[1], 2)
    lead.reduce_near()
    rest.reduce_near()
    upper.spread()
    lower.spread()
    lead.reduce_far()
    rest.reduce_far()
    upper.reduce_near()
    lower.reduce_near()
    lead.hand_back()
    rest.hand_back()
    upper.reduce_far()
    lower.reduce_far()

    scale = 1.0 / (rows * RING)
    r, c = places()
    lead.arrive()
    big[:BLOCK, :BLOCK] = jnp.where(r <= c, lead.get(0) * scale, 0.0)

    def go_on(j):
        if j == 0:
            rest.arrive()
            first, _, third = unfold(lead.get(0), rest.get(0))
            for (i, j), value in zip(
                    ((1, 1), (2, 2), (0, 1), (0, 2), (1, 2)),
                    (first, third, rest.get(1), rest.get(2), rest.get(3))):
                big[i * BLOCK:(i + 1) * BLOCK, j * BLOCK:(j + 1) * BLOCK] = value * scale
            upper.hand_back()
        elif j == 1:
            lower.hand_back()

    eliminate(big, n, work, inverse, between=go_on)
    e = big[:, cols:]
    e_high, e_low = pair(e)
    little[...] = jnp.zeros_like(little)

    def meet(stream, half):
        stream.arrive()
        some = jnp.concatenate([stream.get(j) for j in range(n)], axis=1)
        picked = pl.ds(half * BLOCK, BLOCK)
        solved[picked, :] = mul(some, e, NT)
        return solved[picked, :]

    top = meet(upper, 0)
    little[:BLOCK, :BLOCK] = mul(top, top, NT)

    def second(j):
        if j == 0:
            low = meet(lower, 1)
            little[:BLOCK, BLOCK:keys] = mul(solved[:BLOCK, :], low, NT)
            little[BLOCK:, BLOCK:keys] = mul(low, low, NT)

    few = rows // m // 4

    def slice_of_q(j, step):
        part = pl.ds(pl.multiple_of((j * 4 + step) * few, few), few)
        x = xp_ref[part, :]
        value = mul(x, e_high, NT, False) + mul(x, e_low, NT, False)
        q_ref[part, :] = value
        high, low = pair(value)
        high_ref[part, :] = high
        low_ref[part, :] = low

    eliminate(little, m, work, inverse, right=solved, between=second, beside=slice_of_q)
    right_ref[...] = mul(little[:, keys:], solved[...], TN)
    for stream in (lead, rest, upper, lower):
        stream.drain()


def on_device(samples, column_order, skeleton):
    _, rows, cols = samples.shape
    keys = skeleton.shape[1]
    n, m = cols // BLOCK, keys // BLOCK
    whole = pl.BlockSpec(memory_space=VMEM)
    outside = pl.BlockSpec(memory_space=pltpu.HBM)
    shape = jax.ShapeDtypeStruct
    q, high, low, right = pl.pallas_call(
        factor,
        out_shape=(
            shape((rows, cols), F32), shape((rows, cols), BF16), shape((rows, cols), BF16), shape((keys, cols), F32)),
        in_specs=[outside] * 3,
        out_specs=(whole,) * 4,
        scratch_shapes=room_of(1) + room_of(n * (n + 1) // 2 - 2) + room_of(n) * m + [
            VMEM((cols, 2 * cols), F32), VMEM((keys, 2 * keys), F32), VMEM((keys, cols), F32),
            VMEM((rows, cols), BF16), VMEM((rows, cols), BF16),
            VMEM((1, cols), jnp.int32), VMEM((1, keys), jnp.int32),
            VMEM((BLOCK + PANEL, 2 * BLOCK), F32), VMEM((BLOCK, BLOCK), F32),
        ] + [pltpu.SemaphoreType.DMA((56,))] * 2 + [pltpu.SemaphoreType.DMA((3,)), pltpu.SemaphoreType.REGULAR((2,))],
        compiler_params=pltpu.CompilerParams(
            collective_id=0, has_side_effects=True, vmem_limit_bytes=24 * 2 ** 20),
    )(*[pltpu.with_memory_space_constraint(v, pltpu.HBM) for v in (samples[0], column_order, skeleton)])
    q_factor, interp = pl.pallas_call(
        finish,
        out_shape=(shape((rows, cols), F32), shape((rows, keys), BF16)),
        in_specs=[whole] * 4,
        out_specs=(outside, outside),
        scratch_shapes=[VMEM((rows, keys), BF16), pltpu.SemaphoreType.DMA((5,))],
        compiler_params=pltpu.CompilerParams(vmem_limit_bytes=16 * 2 ** 20),
    )(q, high, low, right)
    return q_factor[None], interp[None]


def solution(mesh):
    placed = (P("node", "row", None), P("node", None), P("node", None))
    return jax.shard_map(
        on_device,
        mesh=mesh,
        in_specs=placed,
        out_specs=(P("node", "row", None), P("node", "row", None)),
        check_vma=False,
    )
```

time: 75.6 us -> 65 us (0.86)
  Pallas kernels: 74.8 us -> 63.6 us
    pallas_call x2, Pallas kernels: 74.8 us -> 63.6 us  [the longest x1 61.8 us: on_device(): pl.pallas_call(factor, out_shape=(shape((rows, cols), F32), shape((rows,...]
where the time goes in v3:
time: 65 us; the launch traced here: 64.2 us
  Pallas kernels  63.6 us (98%)
    pallas_call x1, Pallas kernels, on_device(): pl.pallas_call(factor, out_shape=(shape((rows, cols), F32), shape((rows,...  61.8 us
    pallas_call x1, Pallas kernels, on_device(): pl.pallas_call(finish, out_shape=(shape((rows, cols), F32), shape((rows,...  1.76 us

profile of v3, /device:TPU:6, one launch (start us, length us, event | category | flops | bytes accessed | tf_op | source)
XLA Modules:
  0.0 64.2 jit_solution(12022502798515721787)
XLA Ops:
  0.6 61.8 %shard_map.50 = (f32[1024,384]{1,0:T(8,128)S(1)}, bf16[1024,384]{1,0:T(8,128)(2,1)S(1)}, bf16[1024,384]{1,0:T(8,128)(2,1)S(1)}, f32[256,384]{1,0:T(8,128)S(1)}) custom-call(bf16[1024,384]{1,0:T(8,128)(2,1)} %bitcast.3, s32[1,384]{1,0:T(1,128)} %order_hbm.1, s32[1,256]{1,0:T(1,128)} %skel_hbm.1), custom_call_target="tpu_custom_call" | custom-call | tf_op jit(solution)/shard_map/pallas_call | solution.py:370
  62.4 1.8 %shard_map.51 = (f32[1024,384]{1,0:T(8,128)}, bf16[1024,256]{1,0:T(8,128)(2,1)}) custom-call(f32[1024,384]{1,0:T(8,128)S(1)} %get-tuple-element.8.q_ref, bf16[1024,384]{1,0:T(8,128)(2,1)S(1)} %get-tuple-element.9.high_ref, bf16[1024,384]{1,0:T(8,128)(2,1)S(1)} %get-tuple-element.10.low_ref, f32[256,384]{1,0:T(8,128)S(1)} %get-tuple-element.11.right_ref), custom_call_target="tpu_custom_call" | custom-call | tf_op jit(solution)/shard_map/pallas_call | solution.py:385

commit v4 on v3

--- a/solution.py
+++ b/solution.py
@@ -27,11 +27,11 @@
 
 
 def mul(a, b, dims, exact=True):
-    return lax.dot_general(
-        a, b, (dims, ((), ())),
-        precision=lax.Precision.HIGHEST if exact else None,
-        preferred_element_type=F32,
-    )
+    if exact:
+        left, right = split(a), split(b)
+        a = jnp.concatenate([left[i].astype(BF16) for i in (0, 0, 1, 0, 1, 2)], axis=dims[0][0])
+        b = jnp.concatenate([right[i].astype(BF16) for i in (0, 1, 0, 2, 1, 0)], axis=dims[1][0])
+    return lax.dot_general(a, b, (dims, ((), ())), preferred_element_type=F32)
 
 
 NN, NT, TN = ((1,), (0,)), ((1,), (1,)), ((0,), (0,))
@@ -289,12 +289,12 @@
     for half, stream in enumerate((upper, lower)):
         for j in range(n):
             stream.put(j, chosen[half * BLOCK:(half + 1) * BLOCK, j * BLOCK:(j + 1) * BLOCK])
+    upper.spread()
     pl.semaphore_wait(known.at[0], 2)
     tell(1, (4, -4))
     pl.semaphore_wait(known.at[1], 2)
     lead.reduce_near()
     rest.reduce_near()
-    upper.spread()
     lower.spread()
     lead.reduce_far()
     rest.reduce_far()

time: 65 us -> 63.9 us (0.983)
  no operation moved by 1% of the time
where the time goes in v4:
time: 63.9 us; the launch traced here: 63.6 us
  Pallas kernels  63 us (99%)
  between operations  0.64 us (1%)
    pallas_call x1, Pallas kernels, on_device(): pl.pallas_call(factor, out_shape=(shape((rows, cols), F32), shape((rows,...  61.2 us
    pallas_call x1, Pallas kernels, on_device(): pl.pallas_call(finish, out_shape=(shape((rows, cols), F32), shape((rows,...  1.75 us

profile of v4, /device:TPU:6, one launch (start us, length us, event | category | flops | bytes accessed | tf_op | source)
XLA Modules:
  0.0 63.6 jit_solution(14918744143918616646)
XLA Ops:
  0.6 61.2 %shard_map.50 = (f32[1024,384]{1,0:T(8,128)S(1)}, bf16[1024,384]{1,0:T(8,128)(2,1)S(1)}, bf16[1024,384]{1,0:T(8,128)(2,1)S(1)}, f32[256,384]{1,0:T(8,128)S(1)}) custom-call(bf16[1024,384]{1,0:T(8,128)(2,1)} %bitcast.3, s32[1,384]{1,0:T(1,128)} %order_hbm.1, s32[1,256]{1,0:T(1,128)} %skel_hbm.1), custom_call_target="tpu_custom_call" | custom-call | tf_op jit(solution)/shard_map/pallas_call | solution.py:370
  61.9 1.7 %shard_map.51 = (f32[1024,384]{1,0:T(8,128)}, bf16[1024,256]{1,0:T(8,128)(2,1)}) custom-call(f32[1024,384]{1,0:T(8,128)S(1)} %get-tuple-element.8.q_ref, bf16[1024,384]{1,0:T(8,128)(2,1)S(1)} %get-tuple-element.9.high_ref, bf16[1024,384]{1,0:T(8,128)(2,1)S(1)} %get-tuple-element.10.low_ref, f32[256,384]{1,0:T(8,128)S(1)} %get-tuple-element.11.right_ref), custom_call_target="tpu_custom_call" | custom-call | tf_op jit(solution)/shard_map/pallas_call | solution.py:385

commit v5 on v4

--- a/solution.py
+++ b/solution.py
@@ -56,7 +56,8 @@
     lane = lax.broadcasted_iota(jnp.int32, (PANEL, BLOCK), 1)
 
     def panel(p, carry):
-        here_a, here_e, last_a, last_e = carry
+        here_a, here_e, last_a, last_e, own, coef = carry
+        own, far = list(own), []
         base = pl.multiple_of(PANEL * p, PANEL)
         at = sub + base
         after = (at + PANEL) & (BLOCK - 1)
@@ -68,37 +69,44 @@
         next_e = work[pl.ds(base + PANEL, PANEL), BLOCK:]
         work[:BLOCK, :] = work[:BLOCK, :] - mul(lhs, rhs, TN, exact=False)
         for k in range(PANEL):
-            coef = take(row(last_a, k), after)
-            next_a = next_a - coef * row(last_a, k)
-            next_e = next_e - coef * row(last_e, k)
-        own = [take(row(here_a, k), at) for k in range(PANEL)]
+            next_a = next_a - coef[k] * row(last_a, k)
+            next_e = next_e - coef[k] * row(last_e, k)
         down = [take(row(here_a, k), after) for k in range(PANEL)]
+        ahead = [take(row(next_a, k), after) for k in range(PANEL)]
+        beyond = [take(row(here_a, k), (at + 2 * PANEL) & (BLOCK - 1)) for k in range(PANEL)]
         for k in range(PANEL):
             scale = lax.rsqrt(row(own[k], k))
-            lo, ln = own[k] * scale, down[k] * scale
+            lo, ln, lb = own[k] * scale, down[k] * scale, beyond[k] * scale
+            far.append(lb)
             for m in range(k + 1, PANEL):
                 s = row(lo, m)
                 own[m] = own[m] - lo * s
                 down[m] = down[m] - ln * s
+                beyond[m] = beyond[m] - lb * s
             ua, ue = row(here_a, k) * scale, row(here_e, k) * scale
             below = jnp.where(sub > k, lo, 0.0)
             here_a = jnp.where(sub == k, ua, here_a - below * ua)
             here_e = jnp.where(sub == k, ue, here_e - below * ue)
             next_a = next_a - ln * ua
             next_e = next_e - ln * ue
+            for m in range(PANEL):
+                ahead[m] = ahead[m] - ln * row(ln, m)
         inverse[pl.ds(base, PANEL), :] = here_e
-        return next_a, next_e, here_a, here_e
+        return next_a, next_e, here_a, here_e, tuple(ahead), tuple(far)
 
     def several(step, carry):
-        if beside is not None:
-            beside(step)
-        for k in range(4):
-            carry = panel(step * 4 + k, carry)
+        for part in range(2):
+            if beside is not None:
+                beside(step * 2 + part)
+            for k in range(4):
+                carry = panel((step * 2 + part) * 4 + k, carry)
         return carry
 
     zero = jnp.zeros((PANEL, BLOCK), F32)
-    first = (work[:PANEL, :BLOCK], work[:PANEL, BLOCK:], zero, zero)
-    lax.fori_loop(0, BLOCK // PANEL // 4, several, first)
+    top = work[:PANEL, :BLOCK]
+    start = tuple(take(row(top, k), sub) for k in range(PANEL))
+    first = (top, work[:PANEL, BLOCK:], zero, zero, start, (zero,) * PANEL)
+    lax.fori_loop(0, BLOCK // PANEL // 8, several, first)
 
 
 def eliminate(both, n, work, inverse, right=None, between=None, beside=None):

time: 63.9 us -> 63 us (0.986)
  Pallas kernels: 63 us -> 62.1 us
    pallas_call x1, Pallas kernels: 61.2 us -> 60.3 us  [on_device(): pl.pallas_call(factor, out_shape=(shape((rows, cols), F32), shape((rows,...]
where the time goes in v5:
time: 63 us; the launch traced here: 62.7 us
  Pallas kernels  62.1 us (99%)
  between operations  0.64 us (1%)
    pallas_call x1, Pallas kernels, on_device(): pl.pallas_call(factor, out_shape=(shape((rows, cols), F32), shape((rows,...  60.3 us
    pallas_call x1, Pallas kernels, on_device(): pl.pallas_call(finish, out_shape=(shape((rows, cols), F32), shape((rows,...  1.75 us

profile of v5, /device:TPU:6, one launch (start us, length us, event | category | flops | bytes accessed | tf_op | source)
XLA Modules:
  0.0 62.7 jit_solution(13101489546743301440)
XLA Ops:
  0.6 60.3 %shard_map.50 = (f32[1024,384]{1,0:T(8,128)S(1)}, bf16[1024,384]{1,0:T(8,128)(2,1)S(1)}, bf16[1024,384]{1,0:T(8,128)(2,1)S(1)}, f32[256,384]{1,0:T(8,128)S(1)}) custom-call(bf16[1024,384]{1,0:T(8,128)(2,1)} %bitcast.3, s32[1,384]{1,0:T(1,128)} %order_hbm.1, s32[1,256]{1,0:T(1,128)} %skel_hbm.1), custom_call_target="tpu_custom_call" | custom-call | tf_op jit(solution)/shard_map/pallas_call | solution.py:378
  61.0 1.7 %shard_map.51 = (f32[1024,384]{1,0:T(8,128)}, bf16[1024,256]{1,0:T(8,128)(2,1)}) custom-call(f32[1024,384]{1,0:T(8,128)S(1)} %get-tuple-element.8.q_ref, bf16[1024,384]{1,0:T(8,128)(2,1)S(1)} %get-tuple-element.9.high_ref, bf16[1024,384]{1,0:T(8,128)(2,1)S(1)} %get-tuple-element.10.low_ref, f32[256,384]{1,0:T(8,128)S(1)} %get-tuple-element.11.right_ref), custom_call_target="tpu_custom_call" | custom-call | tf_op jit(solution)/shard_map/pallas_call | solution.py:393
